TPU v7x, 128 devices: a whole 4x4x4 slice. The times are simulated.
128 devices in a mesh: row: 8 (over y_hi, x), col: 16 (over y_lo, z, core).
Axes of the slice: x: 4, y: 4 (y_hi: 2, y_lo: 2; y = y_hi * 2 + y_lo), z: 4, core: 2. Of those that a mesh axis runs over, the one named last changes fastest.
Arguments:
- front_matrix: float32 [8, 8, 256, 4, 16, 256], P(None, 'row', None, None, 'col'), may hold values from -6 to 6
- swap_rows: int32 [3, 256], replicated, may hold values from 0 to 16383, as said below
- l_inverse: float32 [3, 256, 256], replicated, may hold values from -1 to 1, as said below
- u_inverse: float32 [3, 256, 256], replicated, may hold values from -1 to 1, as said below
- contrib_tiles: float32 [12288, 128, 128], P(('row', 'col')), may hold values from -6 to 6
- tile_owner: int32 [12288, 1], P(('row', 'col')), may hold values from 0 to 127; in each aligned block of 96 rows (0 to 95, 96 to 191, ...) at most 2 rows name the same one
- tile_spot: int32 [12288], P(('row', 'col')), may hold values from 0 to 127
Outputs:
- factored: float32 [8, 8, 256, 4, 16, 256], P(None, 'row', None, None, 'col')
Inputs may be any that keep to these rules, and one draw needn't show every extreme that they name: For every k and j, swap_rows[k, j] is either k * 256 + j or a row of (k + 1) * 256 or more; within one k the entries of the second kind are distinct. Each l_inverse[k] is unit lower triangular. Each u_inverse[k] is upper triangular with a positive diagonal. `tile_owner`: among the 96 tiles held by one device, at most 2 have the same owner; some device's tiles reach that bound.
All inputs are finite; a program needn't handle non-finite values.
Results may differ from a plain program's by a relative error of at most 0.00015.
Values sent between devices are 32-bit elements; how exact they have to be, the bound alone decides.
No kernel may reach another device: no remote copies, remote signals or barrier semaphores. Data moves between devices by JAX's collectives and lax.ppermute only.
A program may use at most 192 MiB of HBM per device.

v0:
```python
import jax
import jax.numpy as jnp
from jax import lax
from jax.sharding import PartitionSpec as P

STEPS = 3
CAP = 2


def packed_total(arrays, axis):
    ends = [0]
    for a in arrays:
        ends.append(ends[-1] + a.size)
    running = lax.psum(jnp.concatenate([a.ravel() for a in arrays]), axis)
    return tuple((running[b:e].reshape(a.shape) for a, b, e in zip(arrays, ends, ends[1:])))


def padded_to(lines, count):
    spare = -lines.shape[0] % count
    if not spare:
        return lines
    return jnp.concatenate([lines, jnp.zeros((spare, *lines.shape[1:]), lines.dtype)])


def broadcast_by_parts(value, axis, root):
    lines = jnp.where(lax.axis_index(axis) == root, value, jnp.zeros_like(value)).reshape(
        -1, *value.shape[1:][-1:]
    )
    padded = padded_to(lines, lax.axis_size(axis))
    own = lax.psum_scatter(padded, axis, scatter_dimension=0, tiled=True)
    return lax.all_gather(own, axis, axis=0, tiled=True)[: len(lines)].reshape(value.shape)


def deliver(contrib_tiles, tile_owner, tile_spot):
    tile_count, tile_edge, unused_edge = contrib_tiles.shape
    row_count = lax.axis_size("row")
    col_count = lax.axis_size("col")
    devices = row_count * col_count
    owners = tile_owner[:, 0]
    matches = (owners[:, None] == jnp.arange(devices, dtype=jnp.int32)[None, :]).astype(jnp.int32)
    slot_rank = jnp.sum((jnp.cumsum(matches, axis=0) - matches) * matches, axis=1)
    slot_index = owners * CAP + slot_rank
    flat_tiles = contrib_tiles.reshape(tile_count, tile_edge * tile_edge)
    sending = (
        jnp.zeros((devices * CAP, tile_edge * tile_edge), jnp.float32)
        .at[slot_index]
        .set(flat_tiles)
    )
    spot_ids = jnp.full((devices * CAP,), -1, jnp.int32).at[slot_index].set(tile_spot)
    received, spot_in = (
        lax.all_to_all(
            sending.reshape(devices, CAP, tile_edge * tile_edge),
            ("row", "col"),
            split_axis=0,
            concat_axis=0,
            tiled=True,
        ),
        lax.all_to_all(
            spot_ids.reshape(devices, CAP), ("row", "col"), split_axis=0, concat_axis=0, tiled=True
        ),
    )
    return (received.reshape(devices * CAP, tile_edge * tile_edge), spot_in.reshape(devices * CAP))


def assemble(matrix, received, spot_in, tile_edge):
    local_rows, local_cols = matrix.shape
    row_tiles = local_rows // tile_edge
    col_tiles = local_cols // tile_edge
    onehot = (
        spot_in[None, :] == jnp.arange(row_tiles * col_tiles, dtype=jnp.int32)[:, None]
    ).astype(jnp.float32)
    assembled = jnp.dot(
        onehot, received, precision=lax.Precision.HIGHEST, preferred_element_type=jnp.float32
    )
    assembled = (
        assembled.reshape(row_tiles, col_tiles, tile_edge, tile_edge)
        .transpose(0, 2, 1, 3)
        .reshape(local_rows, local_cols)
    )
    return matrix + assembled


def local(front_matrix, swap_rows, l_inverse, u_inverse, contrib_tiles, tile_owner, tile_spot):
    precise = lax.Precision.HIGHEST
    block_rows, unused_row, block_width, block_cols, unused_col, unused_width = front_matrix.shape
    row_count = lax.axis_size("row")
    col_count = lax.axis_size("col")
    row_place = lax.axis_index("row")
    col_place = lax.axis_index("col")
    local_rows = block_rows * block_width
    local_cols = block_cols * block_width
    matrix = front_matrix.reshape(local_rows, local_cols)
    index_rows = jnp.arange(local_rows, dtype=jnp.int32)
    index_cols = jnp.arange(local_cols, dtype=jnp.int32)
    global_rows = (
        index_rows // block_width * row_count + row_place
    ) * block_width + index_rows % block_width
    global_cols = (
        index_cols // block_width * col_count + col_place
    ) * block_width + index_cols % block_width
    for window_step in range(STEPS):
        past_row = (window_step + 1) * block_width
        targets = swap_rows[window_step]
        home_block = targets // block_width
        owned_here = home_block % row_count == row_place
        local_index = home_block // row_count * block_width + targets % block_width
        top_root = window_step % row_count
        top_start = window_step // row_count * block_width
        top_slab = matrix[top_start : top_start + block_width]
        picked = jnp.where(owned_here[:, None], matrix[jnp.where(owned_here, local_index, 0)], 0.0)
        top_part = jnp.where(row_place == top_root, top_slab, 0.0)
        chosen, leaving = packed_total((picked, top_part), "row")
        landing = jnp.where(owned_here, local_index, local_rows)
        matrix = matrix.at[landing].set(leaving, mode="drop")
        current_top = matrix[top_start : top_start + block_width]
        matrix = matrix.at[top_start : top_start + block_width].set(
            jnp.where(row_place == top_root, chosen, current_top)
        )
        panel_root = window_step % col_count
        panel_start = window_step // col_count * block_width
        below_mask = (global_rows >= past_row)[:, None]
        right_mask = (global_cols >= past_row)[None, :]
        panel_slab = matrix[:, panel_start : panel_start + block_width]
        lower_part = jnp.where(
            below_mask,
            jnp.dot(
                panel_slab,
                u_inverse[window_step],
                precision=precise,
                preferred_element_type=jnp.float32,
            ),
            0.0,
        )
        lower_part = broadcast_by_parts(lower_part, "col", panel_root)
        upper_part = jnp.where(
            right_mask,
            jnp.dot(
                l_inverse[window_step],
                chosen,
                precision=precise,
                preferred_element_type=jnp.float32,
            ),
            0.0,
        )
        matrix = matrix.at[:, panel_start : panel_start + block_width].set(
            jnp.where(below_mask & (col_place == panel_root), lower_part, panel_slab)
        )
        current_top = matrix[top_start : top_start + block_width]
        matrix = matrix.at[top_start : top_start + block_width].set(
            jnp.where(right_mask & (row_place == top_root), upper_part, current_top)
        )
        matrix = matrix - jnp.dot(
            lower_part, upper_part, precision=precise, preferred_element_type=jnp.float32
        )
    received, spot_in = deliver(contrib_tiles, tile_owner, tile_spot)
    matrix = assemble(matrix, received, spot_in, contrib_tiles.shape[1])
    return matrix.reshape(front_matrix.shape)


def solution(mesh):
    placed = (
        P(None, "row", None, None, "col", None),
        P(),
        P(),
        P(),
        P(("row", "col"), None, None),
        P(("row", "col"), None),
        P(("row", "col")),
    )
    return jax.shard_map(
        local,
        mesh=mesh,
        in_specs=placed,
        out_specs=P(None, "row", None, None, "col", None),
        check_vma=False,
    )
```

profile of v0, /device:TPU:30, one launch (start us, length us, event | category | flops | bytes accessed | tf_op | source)
XLA Modules:
  0.0 957.2 jit_solution(2932770433654854582)
XLA Ops:
  6.5 0.8 and_select_fusion.3
  7.4 0.8 fusion.79
  8.2 26.7 %reduce.23 = f32[8,256,4,256]{3,2,1,0:T(4,128)} reduce(f32[8,1,256,4,1,256]{5,4,3,2,1,0:T(1,128)} %param.25, f32[]{:T(128)} %constant.395), dimensions={1,4}, to_apply=%param.25.reduce_sub_computation | reduce | bytes 16777220 | tf_op args[0]
  34.9 8.7 copy.27
  43.5 2.1 broadcast_select_fusion
  45.7 4.9 gather_fusion
  50.8 0.2 copy.28
  51.0 1.5 pad_maximum_fusion
  52.6 92.6 %all-reduce.4.cloned.1.call-done = f32[524288]{0:T(1024)} async-done(((f32[524288]{0:T(1024)}), f32[524288]{0:T(1024)}) %all-reduce.4.cloned.1.call-update) | async-done | bytes 2097168 | tf_op jit(solution)/shard_map/psum | solution.py:14
  145.2 1.7 fusion.78
  146.9 0.2 reshape.1109
  147.3 8.2 scatter_fusion
  155.4 2.3 fusion.20
  157.8 4.7 fusion.6
  162.6 64.9 %reduce-scatter.4.cloned.1.call-done = f32[128,256]{1,0:T(8,128)} async-done(((f32[2048,256]{1,0:T(8,128)}), f32[128,256]{1,0:T(8,128)}) %reduce-scatter.4.cloned.1.call-update) | async-done | bytes 131088 | tf_op jit(solution)/shard_map/reduce_scatter | solution.py:30
  227.5 0.7 compare_reduce_fusion
  228.3 33.5 %all-gather.4.cloned.1.call-done = f32[2048,256]{1,0:T(8,128)} async-done(((f32[128,256]{1,0:T(8,128)}), f32[2048,256]{1,0:T(8,128)}) %all-gather.4.cloned.1.call-update) | async-done | bytes 2097168 | tf_op jit(solution)/shard_map/all_gather | solution.py:31
  261.7 4.4 fusion.7
  266.1 3.4 fusion.19
  269.5 9.8 %convolution_subtract_fusion.1 = f32[2048,1024]{1,0:T(8,128)S(1)} fusion(f32[2048,1024]{1,0:T(8,128)} %get-tuple-element.141, f32[2048,256]{1,0:T(8,128)S(1)} %copy-done.5, f32[1024,256]{0,1:T(8,128)S(1)} %get-tuple-element.142), kind=kOutput, calls=%fused_computation.14 | convolution fusion | flops 6444548096 | bytes 19922944 | tf_op jit(solution)/shard_map/dot_general | solution.py:152
  279.4 3.4 copy-done.1
  282.9 0.2 copy.30
  283.1 5.0 gather_fusion.1
  288.2 0.2 copy.29
  288.4 1.4 pad_maximum_fusion.1
  289.9 90.9 %all-reduce.6.cloned.1.call-done = f32[524288]{0:T(1024)} async-done(((f32[524288]{0:T(1024)}), f32[524288]{0:T(1024)}) %all-reduce.6.cloned.1.call-update) | async-done | bytes 2097168 | tf_op jit(solution)/shard_map/psum | solution.py:14
  380.9 1.7 fusion.77
  382.6 0.2 reshape.1117
  382.9 8.5 scatter_fusion.1
  391.4 2.3 fusion.17
  393.8 4.8 fusion.5
  398.6 64.7 %reduce-scatter.6.cloned.1.call-done = f32[128,256]{1,0:T(8,128)} async-done(((f32[2048,256]{1,0:T(8,128)}), f32[128,256]{1,0:T(8,128)}) %reduce-scatter.6.cloned.1.call-update) | async-done | bytes 131088 | tf_op jit(solution)/shard_map/reduce_scatter | solution.py:30
  463.4 34.0 %all-gather.6.cloned.1.call-done = f32[2048,256]{1,0:T(8,128)} async-done(((f32[128,256]{1,0:T(8,128)}), f32[2048,256]{1,0:T(8,128)}) %all-gather.6.cloned.1.call-update) | async-done | bytes 2097168 | tf_op jit(solution)/shard_map/all_gather | solution.py:31
  497.4 4.2 fusion.8
  501.6 3.4 fusion.16
  505.0 9.8 %convolution_subtract_fusion = f32[2048,1024]{1,0:T(8,128)S(1)} fusion(f32[2048,1024]{1,0:T(8,128)} %get-tuple-element.143, f32[2048,256]{1,0:T(8,128)S(1)} %copy-done.4, f32[1024,256]{0,1:T(8,128)S(1)} %get-tuple-element.144), kind=kOutput, calls=%fused_computation.13 | convolution fusion | flops 6444548096 | bytes 19922944 | tf_op jit(solution)/shard_map/dot_general | solution.py:152
  514.9 3.2 copy-done
  518.2 0.2 copy.32
  518.4 5.0 gather_fusion.2
  523.5 0.2 copy.31
  523.7 1.5 pad_maximum_fusion.2
  525.4 0.2 select_reduce_fusion
  525.6 1.0 scatter_custom_fusion.3
  526.6 0.8 all_to_all.9
  527.4 8.9 all-to-all-start
  536.3 16.6 %scatter_custom_fusion.4 = f32[256,16384]{1,0:T(8,128)} fusion(s32[96]{0:T(128)S(1)} %fusion.70, f32[]{:T(128)} %constant.384.clone.1, f32[12,8,128,128]{3,2,1,0:T(8,128)} %bitcast.136), kind=kCustom, calls=%fused_computation.9 | custom fusion | bytes 23068676 | tf_op jit(solution)/shard_map/scatter | solution.py:47
  552.9 20.1 %reshape.1077 = f32[128,2,16384]{2,1,0:T(2,128)} reshape(f32[256,16384]{1,0:T(8,128)} %scatter_custom_fusion.4) | data formatting | bytes 33554432 | tf_op jit(solution)/shard_map/reshape | solution.py:52
  573.0 10.2 %all-to-all-start.1 = ((f32[128,2,16384]{2,1,0:T(2,128)}), f32[128,2,16384]{2,1,0:T(2,128)}, u32[]{:S(2)}, u32[]{:S(2)}) async-start(f32[128,2,16384]{2,1,0:T(2,128)} %reshape.1077), calls=%async_computation.4 | async-start | bytes 33554432 | tf_op jit(solution)/shard_map/all_to_all | solution.py:51
  583.3 80.9 %all-reduce.8.cloned.1.call-done = f32[524288]{0:T(1024)} async-done(((f32[524288]{0:T(1024)}), f32[524288]{0:T(1024)}) %all-reduce.8.cloned.1.call-update) | async-done | bytes 2097168 | tf_op jit(solution)/shard_map/psum | solution.py:14
  664.2 1.7 fusion.76
  666.2 8.0 scatter_fusion.2
  674.2 2.3 fusion.14
  676.5 4.7 fusion.4
  681.2 0.3 all-gather.8.cloned.1.call-start
  681.5 180.0 %reduce-scatter.8.cloned.1.call-done = f32[128,256]{1,0:T(8,128)} async-done(((f32[2048,256]{1,0:T(8,128)}), f32[128,256]{1,0:T(8,128)}) %reduce-scatter.8.cloned.1.call-update) | async-done | bytes 131088 | tf_op jit(solution)/shard_map/reduce_scatter | solution.py:30
  861.6 0.5 broadcast.1884
  862.1 0.8 reduce.28
  863.1 20.5 %reshape.1078 = f32[256,16384]{1,0:T(8,128)} reshape(f32[128,2,16384]{2,1,0:T(2,128)} %all-to-all-done.1) | data formatting | bytes 33554432 | tf_op jit(solution)/shard_map/reshape | solution.py:62
  883.6 17.5 %copy.21 = f32[16384,256]{1,0:T(8,128)} copy(f32[16384,256]{0,1:T(8,128)} %bitcast.132) | data formatting | bytes 33554432 | tf_op jit(solution)/shard_map/dot_general | solution.py:72
  901.2 15.0 %fusion.33 = f32[16,8,128,128]{3,1,2,0:T(8,128)} fusion(f32[128,128,256,1]{2,1,0,3:T(8,128)} %bitcast.134, s32[16,8]{1,0:T(8,128)S(1)} %multiply_add_fusion, s32[256]{0:T(256)S(1)} %eq.161), kind=kOutput, calls=%fused_computation.68 | convolution fusion | flops 6442483712 | bytes 25167360 | tf_op jit(solution)/shard_map/dot_general | solution.py:72
  916.1 4.5 fusion.9
  920.7 3.9 fusion.13
  924.6 12.3 %bitcast_add_fusion = f32[2048,1024]{1,0:T(8,128)} fusion(f32[256,8,8,128]{3,2,1,0:T(8,128)S(1)} %bitcast.135, f32[2048,1024]{1,0:T(8,128)} %get-tuple-element.145, f32[2048,256]{1,0:T(8,128)S(1)} %copy-done.3, f32[1024,256]{0,1:T(8,128)S(1)} %get-tuple-element.146), kind=kOutput, calls=%fused_computation.8 | convolution fusion | flops 6446645248 | bytes 28311552 | tf_op jit(solution)/shard_map/dot_general | solution.py:152
  936.8 13.5 %reshape.1147 = f32[8,1,256,4,1,256]{5,4,3,2,1,0:T(1,128)} reshape(f32[2048,1024]{1,0:T(8,128)} %bitcast_add_fusion) | data formatting | bytes 16777216 | tf_op jit(solution)/shard_map/reshape | solution.py:157
  (70 shorter events, 2.4 us)
Async XLA Ops:
  6.5 138.7 %all-reduce.4.cloned.1.call-start = ((), (), s32[]{:S(2)}) async-start(), calls=%async_computation.5 | async-start | bytes 4194304 | tf_op jit(solution)/shard_map/psum | solution.py:14
  52.5 174.9 %reduce-scatter.4.cloned.1.call-start = ((), (), s32[]{:S(2)}) async-start(), calls=%async_computation.6 | async-start | bytes 2228224 | tf_op jit(solution)/shard_map/reduce_scatter | solution.py:30
  162.5 99.2 %all-gather.4.cloned.1.call-start = ((), (), s32[]{:S(2)}) async-start(), calls=%async_computation.7 | async-start | bytes 2228224 | tf_op jit(solution)/shard_map/all_gather | solution.py:31
  227.4 153.4 %all-reduce.6.cloned.1.call-start = ((), (), s32[]{:S(2)}) async-start(), calls=%async_computation.8 | async-start | bytes 4194304 | tf_op jit(solution)/shard_map/psum | solution.py:14
  261.7 7.8 copy-start.5
  279.4 3.4 copy-start.1
  289.9 173.4 %reduce-scatter.6.cloned.1.call-start = ((), (), s32[]{:S(2)}) async-start(), calls=%async_computation.9 | async-start | bytes 2228224 | tf_op jit(solution)/shard_map/reduce_scatter | solution.py:30
  398.5 98.9 %all-gather.6.cloned.1.call-start = ((), (), s32[]{:S(2)}) async-start(), calls=%async_computation.10 | async-start | bytes 2228224 | tf_op jit(solution)/shard_map/all_gather | solution.py:31
  463.3 200.9 %all-reduce.8.cloned.1.call-start = ((), (), s32[]{:S(2)}) async-start(), calls=%async_computation.11 | async-start | bytes 4194304 | tf_op jit(solution)/shard_map/psum | solution.py:14
  497.4 7.6 copy-start.4
  514.9 3.2 copy-start
  518.4 6.8 copy-start.6
  527.4 45.6 %all-to-all-start = ((s32[128,1,2]{2,1,0:T(1,128)}), s32[128,1,2]{2,1,0:T(1,128)S(1)}, u32[]{:S(2)}, u32[]{:S(2)}) async-start(s32[128,1,2]{2,1,0:T(1,128)} %bitcast.25), calls=%async_computation.3 | async-start | bytes 131072 | tf_op jit(solution)/shard_map/all_to_all | solution.py:58
  573.0 290.1 %all-to-all-start.1 = ((f32[128,2,16384]{2,1,0:T(2,128)}), f32[128,2,16384]{2,1,0:T(2,128)}, u32[]{:S(2)}, u32[]{:S(2)}) async-start(f32[128,2,16384]{2,1,0:T(2,128)} %reshape.1077), calls=%async_computation.4 | async-start | bytes 33554432 | tf_op jit(solution)/shard_map/all_to_all | solution.py:51
  583.2 278.3 %reduce-scatter.8.cloned.1.call-start = ((), (), s32[]{:S(2)}) async-start(), calls=%async_computation.12 | async-start | bytes 2228224 | tf_op jit(solution)/shard_map/reduce_scatter | solution.py:30
  681.2 234.9 %all-gather.8.cloned.1.call-start = ((), (), s32[]{:S(2)}) async-start(), calls=%async_computation.13 | async-start | bytes 2228224 | tf_op jit(solution)/shard_map/all_gather | solution.py:31
  916.1 8.4 copy-start.2
  916.1 8.4 copy-start.3
Sparse Core Ops, SparseCore 0:
  52.6 92.5 all-reduce.3
  162.6 64.7 reduce-scatter.3
  229.1 32.5 all-gather.3
  290.0 90.8 all-reduce.5
  398.7 64.5 reduce-scatter.5
  464.8 32.5 all-gather.5
  525.3 138.8 all-reduce.7
  681.4 180.1 reduce-scatter.7
  863.3 31.6 all-gather.7
where the time goes:
time: 967 us; the launch traced here: 957 us
  waiting for transfers between devices  642 us (66%)
  local copies, waits for them, and re-layouts  153 us (16%)
  matrix products  71.8 us (7%)
  other arithmetic  56.9 us (6%)
  starting transfers between devices  19.6 us (2%)
  between operations  14 us (1%)
    reduce_scatter x3, waiting for transfers between devices, broadcast_by_parts(): own = lax.psum_scatter(padded, axis, scatter_dimension=0, tiled=True)  310 us
    psum x3, waiting for transfers between devices, packed_total(): running = lax.psum(jnp.concatenate([a.ravel() for a in arrays]), axis)  264 us
    all_gather x3, waiting for transfers between devices, broadcast_by_parts(): lax.all_gather(own, axis, axis=0, tiled=True)[:len(lines)]  67.4 us
    dot_general x3, matrix products, local(): jnp.dot(lower_part, upper_part, precision=precise, preferred_element_type...  31.9 us
    unnamed x6, other arithmetic  27.3 us
    scatter x3, local copies, waits for them, and re-layouts, local(): matrix = matrix.at[landing].set(leaving, mode='drop')  24.7 us
    reshape x1, local copies, waits for them, and re-layouts, deliver(): received.reshape(devices * CAP, tile_edge * tile_edge)  20.5 us
    reshape x1, local copies, waits for them, and re-layouts, deliver(): sending.reshape(devices, CAP, tile_edge * tile_edge)  20.1 us
  transfers between devices with their start and end apart: 11, of which 8 were waited for; matrix products, arithmetic and copies ran while one was open for 12% of the time, Pallas kernels for 0%

commit v1 on v0

--- a/solution.py
+++ b/solution.py
@@ -5,6 +5,11 @@
 
 STEPS = 3
 CAP = 2
+
+
+def gather_over(value, axis, dim):
+    stack = jnp.stack([value] * lax.axis_size(axis))
+    return jnp.concatenate(lax.all_to_all(stack, axis, 0, 0), axis=dim)
 
 
 def packed_total(arrays, axis):
@@ -28,7 +33,7 @@
     )
     padded = padded_to(lines, lax.axis_size(axis))
     own = lax.psum_scatter(padded, axis, scatter_dimension=0, tiled=True)
-    return lax.all_gather(own, axis, axis=0, tiled=True)[: len(lines)].reshape(value.shape)
+    return gather_over(own, axis, 0)[: len(lines)].reshape(value.shape)
 
 
 def deliver(contrib_tiles, tile_owner, tile_spot):

time: 967 us -> 1040 us (1.075)
  local copies, waits for them, and re-layouts: 153 us -> 226 us
  waiting for transfers between devices: 642 us -> 617 us
  starting transfers between devices: 19.6 us -> 34.2 us
    psum x3, waiting for transfers between devices: 264 us -> 392 us  [packed_total(): running = lax.psum(jnp.concatenate([a.ravel() for a in arrays]), axis)]
    reduce_scatter x3, waiting for transfers between devices: 310 us -> 199 us  [broadcast_by_parts(): own = lax.psum_scatter(padded, axis, scatter_dimension=0, tiled=True)]
    all_gather x3 -> x0, waiting for transfers between devices: 67.4 us -> none  [broadcast_by_parts(): lax.all_gather(own, axis, axis=0, tiled=True)[:len(lines)]]
    scatter x3 -> x6, local copies, waits for them, and re-layouts: 24.7 us -> 51.9 us  [local(): matrix = matrix.at[landing].set(leaving, mode='drop')]
    all_to_all x0 -> x3, waiting for transfers between devices: none -> 26 us  [gather_over(): return jnp.concatenate(lax.all_to_all(stack, axis, 0, 0), axis=dim)]
    sub x0 -> x2, local copies, waits for them, and re-layouts: none -> 18.5 us  [local(): matrix - jnp.dot(lower_part, upper_part, precision=precise, preferred_ele...]
    all_to_all x0 -> x3, starting transfers between devices: none -> 14.7 us  [gather_over(): return jnp.concatenate(lax.all_to_all(stack, axis, 0, 0), axis=dim)]
    unnamed x20 -> x14, local copies, waits for them, and re-layouts: 16.3 us -> 23.4 us
  transfers between devices with their start and end apart: 11 -> 11, of which waited for: 8 -> 7; matrix products, arithmetic and copies ran while one was open for 12% -> 17% of each run, Pallas kernels for 0% -> 0%
where the time goes in v1:
time: 1040 us; the launch traced here: 1030 us
  waiting for transfers between devices  617 us (59%)
  local copies, waits for them, and re-layouts  226 us (22%)
  matrix products  77.2 us (7%)
  other arithmetic  57.9 us (6%)
  starting transfers between devices  34.2 us (3%)
  between operations  14.4 us (1%)
    psum x3, waiting for transfers between devices, packed_total(): running = lax.psum(jnp.concatenate([a.ravel() for a in arrays]), axis)  392 us
    reduce_scatter x3, waiting for transfers between devices, broadcast_by_parts(): own = lax.psum_scatter(padded, axis, scatter_dimension=0, tiled=True)  199 us
    scatter x6, local copies, waits for them, and re-layouts, local(): matrix = matrix.at[landing].set(leaving, mode='drop')  51.9 us
    dot_general x3, matrix products, local(): jnp.dot(lower_part, upper_part, precision=precise, preferred_element_type...  32.3 us
    unnamed x1, other arithmetic  26.7 us
    all_to_all x3, waiting for transfers between devices, gather_over(): return jnp.concatenate(lax.all_to_all(stack, axis, 0, 0), axis=dim)  26 us
    unnamed x14, local copies, waits for them, and re-layouts  23.4 us
  transfers between devices with their start and end apart: 11, of which 7 were waited for; matrix products, arithmetic and copies ran while one was open for 17% of the time, Pallas kernels for 0%

profile of v1, /device:TPU:30, one launch (start us, length us, event | category | flops | bytes accessed | tf_op | source)
XLA Modules:
  0.0 1026.4 jit_solution(5834362631079138846)
XLA Ops:
  8.2 26.7 %reduce.23 = f32[8,256,4,256]{3,2,1,0:T(4,128)} reduce(f32[8,1,256,4,1,256]{5,4,3,2,1,0:T(1,128)} %param.25, f32[]{:T(128)} %constant.395), dimensions={1,4}, to_apply=%param.25.reduce_sub_computation | reduce | bytes 16777220 | tf_op args[0]
  34.9 8.7 copy.95
  43.5 2.1 broadcast_select_fusion
  45.7 4.9 gather_fusion
  51.6 1.5 pad_maximum_fusion
  53.2 92.6 %all-reduce.4.cloned.1.call-done = f32[524288]{0:T(1024)} async-done(((f32[524288]{0:T(1024)}), f32[524288]{0:T(1024)}) %all-reduce.4.cloned.1.call-update) | async-done | bytes 2097168 | tf_op jit(solution)/shard_map/psum | solution.py:19
  145.8 1.7 fusion.82
  147.7 8.1 scatter_fusion
  155.8 9.1 copy.57
  165.5 2.3 fusion.24
  167.8 6.6 fusion.6
  174.5 64.9 %reduce-scatter.4.cloned.1.call-done = f32[128,256]{1,0:T(8,128)} async-done(((f32[2048,256]{1,0:T(8,128)}), f32[128,256]{1,0:T(8,128)}) %reduce-scatter.4.cloned.1.call-update) | async-done | bytes 131088 | tf_op jit(solution)/shard_map/reduce_scatter | solution.py:35
  239.4 1.0 copy.58
  240.4 1.6 stack.6
  241.9 4.7 all-to-all-start
  247.5 26.0 %all-to-all-done = f32[16,128,256]{1,2,0:T(8,128)S(1)} async-done(((f32[16,128,256]{1,2,0:T(8,128)}), f32[16,128,256]{1,2,0:T(8,128)S(1)}, u32[]{:S(2)}, u32[]{:S(2)}) %all-to-all-start) | async-done | bytes 2097184 | tf_op jit(solution)/shard_map/all_to_all | solution.py:12
  273.6 3.9 fusion.7
  277.4 4.3 fusion.23
  281.7 11.2 %convolution_subtract_fusion.1 = f32[2048,1024]{0,1:T(8,128)} fusion(f32[2048,1024]{0,1:T(8,128)} %get-tuple-element.141, f32[1024,256]{1,0:T(8,128)S(1)} %get-tuple-element.142, f32[16,128,256]{1,2,0:T(8,128)S(1)} %all-to-all-done), kind=kOutput, calls=%fused_computation.15 | convolution fusion | flops 6444548096 | bytes 19922944 | tf_op jit(solution)/shard_map/dot_general | solution.py:157
  292.9 9.3 copy.65
  302.1 1.3 slice_select_fusion.5
  304.0 4.9 gather_fusion.1
  309.9 1.5 pad_maximum_fusion.1
  311.5 93.0 %all-reduce.6.cloned.1.call-done = f32[524288]{0:T(1024)} async-done(((f32[524288]{0:T(1024)}), f32[524288]{0:T(1024)}) %all-reduce.6.cloned.1.call-update) | async-done | bytes 2097168 | tf_op jit(solution)/shard_map/psum | solution.py:19
  404.5 1.7 fusion.81
  406.3 8.3 scatter_fusion.1
  414.7 9.1 copy.68
  424.3 2.3 fusion.22
  426.7 6.7 fusion.5
  433.3 64.7 %reduce-scatter.6.cloned.1.call-done = f32[128,256]{1,0:T(8,128)} async-done(((f32[2048,256]{1,0:T(8,128)}), f32[128,256]{1,0:T(8,128)}) %reduce-scatter.6.cloned.1.call-update) | async-done | bytes 131088 | tf_op jit(solution)/shard_map/reduce_scatter | solution.py:35
  499.1 1.5 stack.7
  500.6 4.9 all-to-all-start.1
  505.9 16.5 %scatter_custom_fusion.4 = f32[256,16384]{1,0:T(8,128)} fusion(s32[96]{0:T(128)S(1)} %fusion.74, f32[]{:T(128)} %constant.384.clone.1, f32[12,8,128,128]{3,2,1,0:T(8,128)} %bitcast.167), kind=kCustom, calls=%fused_computation.9 | custom fusion | bytes 23068676 | tf_op jit(solution)/shard_map/scatter | solution.py:52
  522.5 20.0 %reshape.1095 = f32[128,2,16384]{2,1,0:T(2,128)} reshape(f32[256,16384]{1,0:T(8,128)} %scatter_custom_fusion.4) | data formatting | bytes 33554432 | tf_op jit(solution)/shard_map/reshape | solution.py:57
  542.5 1.0 scatter_custom_fusion.3
  544.4 9.1 all-to-all-start.3
  553.5 3.9 fusion.8
  557.4 4.3 fusion.21
  561.7 11.2 %convolution_subtract_fusion = f32[2048,1024]{0,1:T(8,128)} fusion(f32[2048,1024]{0,1:T(8,128)} %get-tuple-element.143, f32[1024,256]{1,0:T(8,128)S(1)} %get-tuple-element.144, f32[16,128,256]{1,2,0:T(8,128)S(1)} %all-to-all-done.1), kind=kOutput, calls=%fused_computation.14 | convolution fusion | flops 6444548096 | bytes 19922944 | tf_op jit(solution)/shard_map/dot_general | solution.py:157
  572.8 9.2 copy.76
  582.1 4.9 gather_fusion.2
  587.4 1.3 slice_select_fusion.2
  589.1 1.2 copy.100
  590.8 10.2 all-to-all-start.4
  601.1 1.5 pad_maximum_fusion.2
  602.7 205.9 %all-reduce.8.cloned.1.call-done = f32[524288]{0:T(1024)} async-done(((f32[524288]{0:T(1024)}), f32[524288]{0:T(1024)}) %all-reduce.8.cloned.1.call-update) | async-done | bytes 2097168 | tf_op jit(solution)/shard_map/psum | solution.py:19
  808.6 1.7 fusion.80
  810.4 8.0 scatter_fusion.2
  818.4 9.2 copy.79
  828.0 2.4 fusion.20
  830.5 6.6 fusion.4
  837.1 69.4 %reduce-scatter.8.cloned.1.call-done = f32[128,256]{1,0:T(8,128)} async-done(((f32[2048,256]{1,0:T(8,128)}), f32[128,256]{1,0:T(8,128)}) %reduce-scatter.8.cloned.1.call-update) | async-done | bytes 131088 | tf_op jit(solution)/shard_map/reduce_scatter | solution.py:35
  907.5 1.5 stack.8
  909.0 5.0 all-to-all-start.2
  915.5 20.5 %reshape.1096 = f32[256,16384]{1,0:T(8,128)} reshape(f32[128,2,16384]{2,1,0:T(2,128)} %all-to-all-done.4) | data formatting | bytes 33554432 | tf_op jit(solution)/shard_map/reshape | solution.py:67
  936.0 17.5 %copy.84 = f32[16384,256]{1,0:T(8,128)} copy(f32[16384,256]{0,1:T(8,128)} %bitcast.160) | data formatting | bytes 33554432 | tf_op jit(solution)/shard_map/dot_general | solution.py:77
  953.5 12.1 %fusion.37 = f32[16,8,128,128]{3,1,2,0:T(8,128)S(1)} fusion(f32[128,128,256,1]{2,1,0,3:T(8,128)} %bitcast.165, s32[16,8]{1,0:T(8,128)S(1)} %multiply_add_fusion, s32[256]{0:T(256)S(1)} %eq.161), kind=kOutput, calls=%fused_computation.73 | convolution fusion | flops 6442483712 | bytes 25167360 | tf_op jit(solution)/shard_map/dot_general | solution.py:77
  965.6 5.5 copy.124
  971.1 9.2 copy.91
  980.2 4.1 fusion.9
  984.4 4.3 fusion.19
  988.7 10.0 subtract_add_fusion
  998.7 7.3 copy.103
  1006.0 13.1 %copy.86 = f32[8,1,256,4,1,256]{5,4,3,2,1,0:T(1,128)} copy(f32[8,1,256,4,1,256]{2,0,5,3,4,1:T(8,128)} %bitcast.164) | data formatting | bytes 16777216 | tf_op jit(solution)/shard_map/reshape | solution.py:162
  (82 shorter events, 13.1 us)
Async XLA Ops:
  6.5 139.3 %all-reduce.4.cloned.1.call-start = ((), (), s32[]{:S(2)}) async-start(), calls=%async_computation.8 | async-start | bytes 4194304 | tf_op jit(solution)/shard_map/psum | solution.py:19
  53.1 186.2 %reduce-scatter.4.cloned.1.call-start = ((), (), s32[]{:S(2)}) async-start(), calls=%async_computation.9 | async-start | bytes 2228224 | tf_op jit(solution)/shard_map/reduce_scatter | solution.py:35
  241.9 31.6 %all-to-all-start = ((f32[16,128,256]{1,2,0:T(8,128)}), f32[16,128,256]{1,2,0:T(8,128)S(1)}, u32[]{:S(2)}, u32[]{:S(2)}) async-start(f32[16,128,256]{1,2,0:T(8,128)} %stack.6), calls=%async_computation.1 | async-start | bytes 4194304 | tf_op jit(solution)/shard_map/all_to_all | solution.py:12
  246.7 157.8 %all-reduce.6.cloned.1.call-start = ((), (), s32[]{:S(2)}) async-start(), calls=%async_computation.10 | async-start | bytes 4194304 | tf_op jit(solution)/shard_map/psum | solution.py:19
  311.4 186.7 %reduce-scatter.6.cloned.1.call-start = ((), (), s32[]{:S(2)}) async-start(), calls=%async_computation.11 | async-start | bytes 2228224 | tf_op jit(solution)/shard_map/reduce_scatter | solution.py:35
  426.7 78.9 %copy-start.2 = (s32[96,1]{0,1:T(1,128)S(1)}, s32[96,1]{0,1:T(1,128)}, u32[]{:S(2)}) copy-start(s32[96,1]{0,1:T(1,128)} %param.30) | copy-start | bytes 1156
  500.6 43.8 %all-to-all-start.1 = ((f32[16,128,256]{1,2,0:T(8,128)}), f32[16,128,256]{1,2,0:T(8,128)S(1)}, u32[]{:S(2)}, u32[]{:S(2)}) async-start(f32[16,128,256]{1,2,0:T(8,128)} %stack.7), calls=%async_computation.3 | async-start | bytes 4194304 | tf_op jit(solution)/shard_map/all_to_all | solution.py:12
  544.4 46.4 %all-to-all-start.3 = ((s32[128,1,2]{2,1,0:T(1,128)}), s32[128,1,2]{2,1,0:T(1,128)S(1)}, u32[]{:S(2)}, u32[]{:S(2)}) async-start(s32[128,1,2]{2,1,0:T(1,128)} %bitcast.25), calls=%async_computation.6 | async-start | bytes 131072 | tf_op jit(solution)/shard_map/all_to_all | solution.py:63
  590.8 10.3 %copy-start.1 = (f32[32,8,8,128]{3,1,2,0:T(8,128)S(1)}, f32[32,8,8,128]{3,1,2,0:T(8,128)}, u32[]{:S(2)}) copy-start(f32[32,8,8,128]{3,1,2,0:T(8,128)} %copy.100) | copy-start | bytes 3145732
  590.8 316.7 %all-to-all-start.4 = ((f32[128,2,16384]{2,1,0:T(2,128)}), f32[128,2,16384]{2,1,0:T(2,128)}, u32[]{:S(2)}, u32[]{:S(2)}) async-start(f32[128,2,16384]{2,1,0:T(2,128)} %reshape.1095), calls=%async_computation.7 | async-start | bytes 33554432 | tf_op jit(solution)/shard_map/all_to_all | solution.py:56
  601.0 207.5 %all-reduce.8.cloned.1.call-start = ((), (), s32[]{:S(2)}) async-start(), calls=%async_computation.12 | async-start | bytes 4194304 | tf_op jit(solution)/shard_map/psum | solution.py:19
  602.6 303.9 %reduce-scatter.8.cloned.1.call-start = ((), (), s32[]{:S(2)}) async-start(), calls=%async_computation.13 | async-start | bytes 2228224 | tf_op jit(solution)/shard_map/reduce_scatter | solution.py:35
  909.0 71.2 %all-to-all-start.2 = ((f32[16,128,256]{1,2,0:T(8,128)}), f32[16,128,256]{1,2,0:T(8,128)S(1)}, u32[]{:S(2)}, u32[]{:S(2)}) async-start(f32[16,128,256]{1,2,0:T(8,128)} %stack.8), calls=%async_computation.5 | async-start | bytes 4194304 | tf_op jit(solution)/shard_map/all_to_all | solution.py:12
  980.2 8.5 copy-start
Sparse Core Ops, SparseCore 0:
  53.2 92.5 all-reduce.3
  174.6 64.7 reduce-scatter.3
  311.5 92.9 all-reduce.5
  433.5 64.5 reduce-scatter.5
  604.1 204.4 all-reduce.7
  837.2 69.1 reduce-scatter.7
